TPU v7x, 8 devices: a whole 2x2x1 slice. The times are simulated.
8 devices in a mesh: dp: 1 (over z), sp: 8 (over y, x, core).
Axes of the slice: x: 2, y: 2, z: 1, core: 2. Of those that a mesh axis runs over, the one named last changes fastest.
Arguments:
- hidden_in: bfloat16 [4, 1024, 4096], P('dp', 'sp')
- pos_ids: int32 [4, 1024], P('dp', 'sp')
- block_pos: int32 [4, 1024], P('dp', 'sp')
- prefix_len: int32 [4], P('dp')
- ln_gamma: bfloat16 [4096], replicated
- ln_beta: bfloat16 [4096], replicated
- w_qkv: bfloat16 [4096, 12288], replicated
- b_qkv: bfloat16 [12288], replicated
- w_o: bfloat16 [4096, 4096], replicated
- b_o: bfloat16 [4096], replicated
- grad_out: bfloat16 [4, 1024, 4096], P('dp', 'sp')
Outputs:
- output 1: bfloat16 [4, 1024, 4096], P('dp', 'sp')
- output 2: bfloat16 [4, 1024, 4096], P('dp', 'sp')
- output 3: float32 [4096], P('dp')
- output 4: float32 [4096], P('dp')
- output 5: float32 [4096, 12288], P('dp')
- output 6: float32 [12288], P('dp')
- output 7: float32 [4096, 4096], P('dp')
- output 8: float32 [4096], P('dp')
All inputs are finite; a program needn't handle non-finite values.
Results may differ from a plain program's by a relative error of at most 0.0110327.
Values are sent between devices in bfloat16 or wider.
A program may use at most 1.75 GiB of HBM per device.

v0:
```python
import math
import jax
import jax.numpy as jnp
from jax import lax
from jax.sharding import PartitionSpec as P

HEAD = 128
QUARTER = 32
ALPHA = math.sqrt(56.0)
LN_EPS = 1e-5
ROT_BASE = 10000.0
SCALE = 1.0 / math.sqrt(HEAD)
MASK_FILL = -1e30


def query_block(n_query, row_count):
    blk_size = math.gcd(n_query, 512)
    while blk_size > 8 and blk_size * row_count > 1024:
        blk_size = blk_size // 2
    return blk_size


def layer_norm(x_val, ln_gain, ln_shift):
    row_mean = jnp.mean(x_val, axis=-1, keepdims=True)
    centered = x_val - row_mean
    row_var = jnp.mean(centered * centered, axis=-1, keepdims=True)
    return centered * lax.rsqrt(row_var + LN_EPS) * ln_gain + ln_shift


def rope_tables(pos_ids, block_pos):
    inv_freq = ROT_BASE ** (-jnp.arange(QUARTER, dtype=jnp.float32) / QUARTER)
    angles = jnp.stack([pos_ids, block_pos], axis=-1).astype(jnp.float32)[..., None] * inv_freq
    return jnp.cos(angles), jnp.sin(angles)


def rotate_slots(vals, cos_tab, sin_tab, direction):
    shaped = vals.reshape(vals.shape[:4] + (2, 2, QUARTER))
    half_a = shaped[..., 0, :]
    half_b = shaped[..., 1, :]
    rot_mask = jnp.array([1.0, 1.0, 0.0], jnp.float32)[:, None, None]
    cos_b = cos_tab[:, :, None, None] * rot_mask + (1.0 - rot_mask)
    sin_b = direction * sin_tab[:, :, None, None] * rot_mask
    rotated = jnp.stack([half_a * cos_b - half_b * sin_b, half_b * cos_b + half_a * sin_b], axis=-2)
    return rotated.reshape(vals.shape)


def masked_scores(q_blk, key_rot, prefix_len, row_start):
    scores = jnp.einsum('bqhd,bkhd->bhqk', q_blk, key_rot, preferred_element_type=jnp.float32) * SCALE
    query_idx = row_start + jnp.arange(q_blk.shape[1])
    key_idx = jnp.arange(key_rot.shape[1])
    allowed = (key_idx[None, None, :] < prefix_len[:, None, None]) | (key_idx[None, None, :] <= query_idx[None, :, None])
    return jnp.where(allowed[:, None], scores, MASK_FILL)


def attention_forward(queries, key_rot, values, prefix_len, row_base, q_size):
    def one_block(blk_index):
        row_start = blk_index * q_size
        q_blk = lax.dynamic_slice_in_dim(queries, row_start, q_size, axis=1)
        scores = masked_scores(q_blk, key_rot, prefix_len, row_base + row_start)
        row_max = jnp.max(scores, axis=-1, keepdims=True)
        exp_scores = jnp.exp(scores - row_max)
        row_sum = jnp.sum(exp_scores, axis=-1, keepdims=True)
        probs = (exp_scores / row_sum).astype(jnp.bfloat16)
        ctx_blk = jnp.einsum('bhqk,bkhd->bqhd', probs, values, preferred_element_type=jnp.float32)
        return ctx_blk.astype(jnp.bfloat16), (row_max + jnp.log(row_sum))[..., 0]
    ctx_blocks, log_sums = lax.map(one_block, jnp.arange(queries.shape[1] // q_size))
    return jnp.moveaxis(ctx_blocks, 0, 1).reshape(queries.shape), log_sums


def attention_backward(queries, key_rot, values, ctx, d_ctx, log_sums, prefix_len, row_base, q_size):
    def one_block(carry, block_in):
        dk_acc, dv_acc = carry
        blk_index, blk_lse = block_in
        row_start = blk_index * q_size
        q_blk = lax.dynamic_slice_in_dim(queries, row_start, q_size, axis=1)
        ctx_blk = lax.dynamic_slice_in_dim(ctx, row_start, q_size, axis=1)
        grad_blk = lax.dynamic_slice_in_dim(d_ctx, row_start, q_size, axis=1)
        scores = masked_scores(q_blk, key_rot, prefix_len, row_base + row_start)
        probs = jnp.exp(scores - blk_lse[..., None])
        dv_acc = dv_acc + jnp.einsum('bhqk,bqhd->bkhd', probs.astype(jnp.bfloat16), grad_blk, preferred_element_type=jnp.float32)
        d_prob = jnp.einsum('bqhd,bkhd->bhqk', grad_blk, values, preferred_element_type=jnp.float32)
        row_delta = jnp.einsum('bqhd,bqhd->bhq', grad_blk, ctx_blk, preferred_element_type=jnp.float32)
        d_score = (probs * (d_prob - row_delta[..., None]) * SCALE).astype(jnp.bfloat16)
        dq_blk = jnp.einsum('bhqk,bkhd->bqhd', d_score, key_rot, preferred_element_type=jnp.float32)
        dk_acc = dk_acc + jnp.einsum('bhqk,bqhd->bkhd', d_score, q_blk, preferred_element_type=jnp.float32)
        return (dk_acc, dv_acc), dq_blk.astype(jnp.bfloat16)
    zero_acc = jnp.zeros(key_rot.shape, jnp.float32)
    n_blocks = queries.shape[1] // q_size
    (dk_sum, dv_sum), dq_blocks = lax.scan(one_block, (zero_acc, zero_acc), (jnp.arange(n_blocks), log_sums))
    return jnp.moveaxis(dq_blocks, 0, 1).reshape(queries.shape), dk_sum, dv_sum


def solution(mesh):
    tok_spec = P('dp', 'sp', None)
    pos_spec = P('dp', 'sp')
    in_specs = (tok_spec, pos_spec, pos_spec, P('dp'), P(), P(), P(), P(), P(), P(), tok_spec)
    out_specs = (tok_spec, tok_spec, P('dp'), P('dp'), P('dp', None), P('dp'), P('dp', None), P('dp'))

    def device_step(hidden_in, pos_ids, block_pos, prefix_len, ln_gamma, ln_beta, w_qkv, b_qkv, w_o, b_o, grad_out):
        batch, local_len, hidden = hidden_in.shape
        heads = hidden // HEAD
        normed_f, norm_vjp = jax.vjp(layer_norm, hidden_in.astype(jnp.float32), ln_gamma.astype(jnp.float32), ln_beta.astype(jnp.float32))
        normed = normed_f.astype(jnp.bfloat16)
        pre_qkv = jnp.einsum('bsh,hc->bsc', normed, w_qkv, preferred_element_type=jnp.float32) + b_qkv.astype(jnp.float32)
        cos_tab, sin_tab = rope_tables(pos_ids, block_pos)
        qkv_tok = rotate_slots(pre_qkv.reshape(batch, local_len, heads, 3, HEAD), cos_tab, sin_tab, 1.0).astype(jnp.bfloat16)
        qkv_head = lax.all_to_all(qkv_tok, 'sp', 2, 1, tiled=True)
        queries = qkv_head[:, :, :, 0]
        key_rot = qkv_head[:, :, :, 1]
        values = qkv_head[:, :, :, 2]
        q_size = query_block(queries.shape[1], batch * queries.shape[2])
        ctx_head, log_sums = attention_forward(queries, key_rot, values, prefix_len, 0, q_size)
        ctx_tok = lax.all_to_all(ctx_head, 'sp', 1, 2, tiled=True).reshape(batch, local_len, hidden)
        out_f = jnp.einsum('bsh,hc->bsc', ctx_tok, w_o, preferred_element_type=jnp.float32) + b_o.astype(jnp.float32)
        hidden_out = (ALPHA * normed.astype(jnp.float32) + out_f).astype(jnp.bfloat16)

        grad_bo = jnp.sum(grad_out.astype(jnp.float32), axis=(0, 1))
        grad_wo = jnp.einsum('bsh,bsc->hc', ctx_tok, grad_out, preferred_element_type=jnp.float32)
        d_ctx_tok = jnp.einsum('bsc,hc->bsh', grad_out, w_o, preferred_element_type=jnp.float32).astype(jnp.bfloat16)
        d_ctx_head = lax.all_to_all(d_ctx_tok.reshape(batch, local_len, heads, HEAD), 'sp', 2, 1, tiled=True)
        d_q, dk_sum, dv_sum = attention_backward(queries, key_rot, values, ctx_head, d_ctx_head, log_sums, prefix_len, 0, q_size)
        grad_head = jnp.stack([d_q, dk_sum.astype(jnp.bfloat16), dv_sum.astype(jnp.bfloat16)], axis=3)
        grad_tok = lax.all_to_all(grad_head, 'sp', 1, 2, tiled=True)
        g_pre = rotate_slots(grad_tok.astype(jnp.float32), cos_tab, sin_tab, -1.0).reshape(batch, local_len, 3 * hidden)
        grad_bqkv = jnp.sum(g_pre, axis=(0, 1))
        g_pre_b = g_pre.astype(jnp.bfloat16)
        grad_wqkv = jnp.einsum('bsh,bsc->hc', normed, g_pre_b, preferred_element_type=jnp.float32)
        d_norm = jnp.einsum('bsc,hc->bsh', g_pre_b, w_qkv, preferred_element_type=jnp.float32) + ALPHA * grad_out.astype(jnp.float32)
        d_x, grad_gamma, grad_beta = norm_vjp(d_norm)
        weight_grads = lax.psum((grad_gamma, grad_beta, grad_wqkv, grad_bqkv, grad_wo, grad_bo), 'sp')
        return (hidden_out, d_x.astype(jnp.bfloat16)) + tuple(weight_grads)

    return jax.shard_map(device_step, mesh=mesh, in_specs=in_specs, out_specs=out_specs, check_vma=False)
```

profile of v0, /device:TPU:1, one launch (start us, length us, event | category | flops | bytes accessed | tf_op | source)
XLA Modules:
  0.0 4523.7 jit_solution(12291066519053470215)
XLA Ops:
  7.2 22.7 fusion.64
  45.2 60.2 %fusion.41 = f32[4,128,12288]{2,1,0:T(8,128)} fusion(bf16[4096,12288]{1,0:T(8,128)(2,1)} %param.23, f32[12288]{0:T(1024)S(1)} %convert_element_type.96, bf16[4,128,4096]{2,1,0:T(8,128)(2,1)S(1)} %copy-done.4, f32[4096]{0:T(1024)S(1)} %convert_element_type.93, f32[4096]{0:T(1024)S(1)} %convert_element_type.92, f32[4,128]{1,0:T(4,128)S(1)} %fusion.69, ...), kind=kOutput, calls=%fused_computation.64 | convolution fusion | flops 51558481920 | bytes 130109440 | tf_op jit(solution)/shard_map/bsh,hc->bsc/dot_general | solution.py:104
  105.5 24.7 copy.75
  131.7 10.1 subtract_convert_fusion
  148.9 15.7 all-to-all-start
  169.4 130.4 %all-to-all-done = bf16[4,128,32,3,128]{1,4,3,0,2:T(8,128)(2,1)} async-done(((bf16[4,128,32,3,128]{1,4,3,0,2:T(8,128)(2,1)}), bf16[4,128,32,3,128]{1,4,3,0,2:T(8,128)(2,1)}, u32[]{:S(2)}, u32[]{:S(2)}) %all-to-all-start) | async-done | bytes 12582944 | tf_op jit(solution)/shard_map/all_to_all | solution.py:107
  299.8 16.6 copy.79
  316.4 9.2 slice_bitcast_fusion
  325.6 147.1 %while.27 = (s32[]{:T(128)}, bf16[16,4,64,4,128]{4,2,3,1,0:T(8,128)(2,1)}, f32[16,4,4,64]{3,2,1,0:T(4,128)S(1)}, s32[4]{0:T(128)S(1)}, s32[16]{0:T(128)S(1)}, /*...) while((s32[]{:T(128)}, ...), condition=%wide.region_5.6_spmd, body=%wide.region_2.5_spmd.sunk | while | flops 549915712 | bytes 39506672 | solution.py:66
  472.8 7.8 copy.80
  480.6 10.7 copy.107
  491.3 7.0 all-to-all-start.1
  498.3 495.4 %while.28 = (s32[]{:T(128)}, f32[4,1024,4,128]{1,3,2,0:T(8,128)}, f32[4,1024,4,128]{1,3,2,0:T(8,128)}, bf16[16,4,64,4,128]{4,2,0,3,1:T(8,128)(2,1)}, s32[16]{0:T...) while((s32[]{:T(128)}, f32[4,1024,4,128]{1,3,2,0:T(8,128)}, ...), condition=%wide.region_7.8_spmd.clone, body=%wide.region_6.7_spmd.clone.sunk | while | flops 1363086336 | bytes 161129360 | solution.py:89
  542.4 8.3 bitcast_add_fusion.4
  573.5 8.3 bitcast_add_fusion.4
  604.6 8.3 bitcast_add_fusion.4
  635.7 8.3 bitcast_add_fusion.4
  666.9 8.3 bitcast_add_fusion.4
  698.0 8.3 bitcast_add_fusion.4
  729.2 8.3 bitcast_add_fusion.4
  760.3 8.3 bitcast_add_fusion.4
  791.4 8.3 bitcast_add_fusion.4
  822.6 8.3 bitcast_add_fusion.4
  853.7 8.3 bitcast_add_fusion.4
  884.8 8.3 bitcast_add_fusion.4
  915.9 8.3 bitcast_add_fusion.4
  947.0 8.3 bitcast_add_fusion.4
  978.1 8.3 bitcast_add_fusion.4
  993.7 7.1 copy.87
  1000.8 7.1 copy.86
  1014.4 41.5 copy.88
  1069.7 7.9 reshape.261
  1077.5 117.9 %all-to-all-done.3 = bf16[4,1024,4,3,128]{4,2,0,3,1:T(4,128)(2,1)} async-done(((bf16[4,1024,4,3,128]{4,2,0,3,1:T(4,128)(2,1)}), bf16[4,1024,4,3,128]{4,2,0,3,1:T(4,128)(2,1)}, u32[]{:S(2)}, u32[]{:S(2)}) %all-to-all-start.3) | async-done | bytes 12582944 | tf_op jit(solution)/shard_map/all_to_all | solution.py:123
  1195.5 7.5 copy.89
  1203.0 9.0 convert_bitcast_fusion
  1212.0 24.8 copy.90
  1236.8 15.4 multiply_subtract_fusion
  1252.2 11.5 fusion.40
  1267.9 67.8 %fusion.70 = (f32[4096]{0:T(1024)}, f32[4,128]{1,0:T(4,128)S(1)}, f32[4,128,4096]{2,1,0:T(8,128)}) fusion(f32[4096]{0:T(1024)S(1)} %copy-done.10, f32[4,128]{1,0:T(4,128)S(1)} %copy-done.6, bf16[4,128,4096]{2,1,0:T(8,128)(2,1)} %param.17, bf16[4,128,4096]{2,1,0:T(8,128)(2,1)} %param.27, bf16[4,128,12288]{1,2,0:T(8,128)(2,1)} %bitcast.163, ...), kind=kOutput, calls=%fused_computation.113 | convolution fusion | flops 51558477824 | bytes 130060288 | tf_op jit(solution)/shard_map/bsc,hc->bsh/dot_general | solution.py:128
  1336.5 7.2 fusion.52
  1343.7 30.9 convolution_bitcast_fusion.1
  1375.4 78.0 %convolution_bitcast_fusion = f32[4096,12288]{1,0:T(8,128)} fusion(bf16[4,128,12288]{1,2,0:T(8,128)(2,1)} %bitcast.164, bf16[4,128,4096]{2,1,0:T(8,128)(2,1)} %param.17, f32[4096]{0:T(1024)S(1)} %copy-done.12, f32[4096]{0:T(1024)S(1)} %copy-done.10, f32[4,128]{1,0:T(4,128)S(1)} %copy-done.8, f32[4,128]{1,0:T(4,128)S(1)} %copy-done.6), kind=kOutput, calls=%fused_computation.50 | convolution fusion | flops 51552190464 | bytes 218140672 | tf_op jit(solution)/shard_map/bsh,bsc->hc/dot_general | solution.py:127
  1454.0 27.7 add_convert_fusion.2
  1481.8 7.7 add_convert_fusion.1
  1489.4 650.0 %all-reduce.7.cloned.1.call-done = f32[4096,4096]{1,0:T(8,128)} async-done(((f32[4096,4096]{1,0:T(8,128)}), f32[4096,4096]{1,0:T(8,128)}) %all-reduce.7.cloned.1.call-update) | async-done | bytes 67108880 | tf_op jit(solution)/shard_map/psum | solution.py:130
  2139.4 2199.4 %all-reduce.5.cloned.1.call-done = f32[4096,12288]{1,0:T(8,128)} async-done(((f32[4096,12288]{1,0:T(8,128)}), f32[4096,12288]{1,0:T(8,128)}) %all-reduce.5.cloned.1.call-update) | async-done | bytes 201326608 | tf_op jit(solution)/shard_map/psum | solution.py:130
  4341.4 130.2 %copy.152 = f32[4096,12288]{1,0:T(8,128)} copy(f32[4096,12288]{1,0:T(8,128)} %all-reduce.5.cloned.1.call-done) | data formatting | bytes 402653184
  4472.3 44.1 copy.154
  (667 shorter events, 553.1 us)
Async XLA Ops:
  33.2 115.7 %all-to-all-start.2 = ((bf16[4,128,32,128]{3,1,0,2:T(8,128)(2,1)}), bf16[4,128,32,128]{3,1,0,2:T(8,128)(2,1)}, u32[]{:S(2)}, u32[]{:S(2)}) async-start(bf16[4,128,32,128]{3,1,0,2:T(8,128)(2,1)} %bitcast.157), calls=%async_computation.2 | async-start | bytes 8388608 | tf_op jit(solution)/shard_map/all_to_all | solution.py:120
  105.5 24.7 copy-start.30
  105.5 24.7 copy-start.31
  105.5 25.3 copy-start.32
  105.5 25.3 copy-start.33
  131.7 10.1 copy-start.15
  148.9 151.0 %all-to-all-start = ((bf16[4,128,32,3,128]{1,4,3,0,2:T(8,128)(2,1)}), bf16[4,128,32,3,128]{1,4,3,0,2:T(8,128)(2,1)}, u32[]{:S(2)}, u32[]{:S(2)}) async-start(bf16[4,128,32,3,128]{1,4,3,0,2:T(8,128)(2,1)} %copy.77), calls=%async_computation | async-start | bytes 25165824 | tf_op jit(solution)/shard_map/all_to_all | solution.py:107
  316.4 9.2 copy-start.18
  491.3 564.6 %all-to-all-start.1 = ((bf16[4,1024,4,128]{3,2,0,1:T(4,128)(2,1)}), bf16[4,1024,4,128]{3,2,0,1:T(4,128)(2,1)}, u32[]{:S(2)}, u32[]{:S(2)}) async-start(bf16[4,1024,4,128]{3,2,0,1:T(4,128)(2,1)} %bitcast.156), calls=%async_computation.1 | async-start | bytes 8388608 | tf_op jit(solution)/shard_map/all_to_all | solution.py:113
  508.3 11.4 slice-start
  536.9 13.9 slice-start
  542.4 8.4 copy-start.1
  568.0 13.9 slice-start
  573.5 8.4 copy-start.1
  599.1 13.9 slice-start
  604.6 8.4 copy-start.1
  630.2 13.9 slice-start
  635.7 8.4 copy-start.1
  661.3 13.9 slice-start
  666.8 8.4 copy-start.1
  692.5 13.9 slice-start
  698.0 8.4 copy-start.1
  723.6 13.9 slice-start
  729.1 8.4 copy-start.1
  754.7 13.9 slice-start
  785.9 13.9 slice-start
  791.4 8.4 copy-start.1
  817.0 13.9 slice-start
  848.1 13.9 slice-start
  879.2 13.9 slice-start
  910.3 13.9 slice-start
  915.9 8.4 copy-start.1
  941.5 13.9 slice-start
  972.6 13.9 slice-start
  1055.9 139.6 %all-to-all-start.3 = ((bf16[4,1024,4,3,128]{4,2,0,3,1:T(4,128)(2,1)}), bf16[4,1024,4,3,128]{4,2,0,3,1:T(4,128)(2,1)}, u32[]{:S(2)}, u32[]{:S(2)}) async-start(bf16[4,1024,4,3,128]{4,2,0,3,1:T(4,128)(2,1)} %copy.88), calls=%async_computation.3 | async-start | bytes 25165824 | tf_op jit(solution)/shard_map/all_to_all | solution.py:123
  1060.2 429.3 %all-reduce.9.cloned.1.call-start = ((), (), s32[]{:S(2)}) async-start(), calls=%async_computation.6 | async-start | bytes 196608 | tf_op jit(solution)/shard_map/psum | solution.py:130
  1212.0 24.8 copy-start.16
  1212.0 24.8 copy-start.17
  1252.2 12.9 copy-start.3
  1267.8 67.8 %copy-start.22 = (f32[4,128]{1,0:T(4,128)S(1)}, f32[4,128]{1,0:T(4,128)}, u32[]{:S(2)}) copy-start(f32[4,128]{1,0:T(4,128)} %copy-done.21) | copy-start | bytes 6148
  1267.9 68.6 %copy-start.8 = (f32[4,128]{1,0:T(4,128)S(1)}, f32[4,128]{1,0:T(4,128)}, u32[]{:S(2)}) copy-start(f32[4,128]{1,0:T(4,128)} %copy-done.7) | copy-start | bytes 6148
  1335.7 39.0 copy-start.23
  1343.7 795.7 %all-reduce.7.cloned.1.call-start = ((), (), s32[]{:S(2)}) async-start(), calls=%async_computation.5 | async-start | bytes 134217728 | tf_op jit(solution)/shard_map/psum | solution.py:130
  1374.7 2964.1 %all-reduce.5.cloned.1.call-start = ((), (), s32[]{:S(2)}) async-start(), calls=%async_computation.4 | async-start | bytes 402653184 | tf_op jit(solution)/shard_map/psum | solution.py:130
  1454.0 27.7 copy-start.29
  1454.0 27.7 copy-start.24
  4341.4 130.2 %copy-start.19 = (f32[12288]{0:T(1024)S(1)}, f32[12288]{0:T(1024)}, u32[]{:S(2)}) copy-start(f32[12288]{0:T(1024)} %get-tuple-element.462) | copy-start | bytes 147460
  4472.3 44.1 copy-start.25
  (85 other events, 452.4 us)
Sparse Core Ops, SparseCore 0:
  1343.8 44.4 all-reduce.8
  1392.6 746.7 all-reduce.6
  2143.8 2194.9 all-reduce.4
where the time goes:
time: 4530 us; the launch traced here: 4520 us
  waiting for transfers between devices  3100 us (68%)
  matrix products  798 us (18%)
  local copies, waits for them, and re-layouts  408 us (9%)
  other arithmetic  151 us (3%)
    psum x3, waiting for transfers between devices, device_step(): lax.psum((grad_gamma, grad_beta, grad_wqkv, grad_bqkv, grad_wo, grad_bo),...  2850 us
    unnamed x66, local copies, waits for them, and re-layouts  182 us
    dot_general x32, matrix products, masked_scores(): jnp.einsum('bqhd,bkhd->bhqk', q_blk, key_rot, preferred_element_type=jnp....  160 us
    dot_general x16, matrix products, one_block(): jnp.einsum('bhqk,bqhd->bkhd', d_score, q_blk, preferred_element_type=jnp....  131 us
    all_to_all x1, waiting for transfers between devices, device_step(): qkv_head = lax.all_to_all(qkv_tok, 'sp', 2, 1, tiled=True)  130 us
    all_to_all x1, waiting for transfers between devices, device_step(): grad_tok = lax.all_to_all(grad_head, 'sp', 1, 2, tiled=True)  118 us
  transfers between devices with their start and end apart: 7, of which 4 were waited for; matrix products, arithmetic and copies ran while one was open for 18% of the time, Pallas kernels for 0%

commit v1 on v0

v1 whole, which is shorter than its diff:
```python
import functools
import math
import jax
import jax.numpy as jnp
from jax import lax
from jax.experimental import pallas as pl
from jax.experimental.pallas import tpu as pltpu
from jax.sharding import PartitionSpec as P

HEAD = 128
QUARTER = 32
ALPHA = math.sqrt(56.0)
LN_EPS = 1e-5
ROT_BASE = 10000.0
SCALE = 1.0 / math.sqrt(HEAD)
LOG2E = math.log2(math.e)
MASK_FILL = -1e30
BLK = 256
MIB = 1 << 20
F32 = jnp.float32
BF16 = jnp.bfloat16


def dot(lhs, rhs, lhs_dim, rhs_dim):
    return lax.dot_general(lhs, rhs, (((lhs_dim,), (rhs_dim,)), ((), ())), preferred_element_type=F32)


def cost(flops, nbytes, transcendentals=0):
    return pl.CostEstimate(flops=int(flops), bytes_accessed=int(nbytes), transcendentals=int(transcendentals))


def layer_norm(x_val, ln_gain, ln_shift):
    row_mean = jnp.mean(x_val, axis=-1, keepdims=True)
    centered = x_val - row_mean
    row_var = jnp.mean(centered * centered, axis=-1, keepdims=True)
    return centered * lax.rsqrt(row_var + LN_EPS) * ln_gain + ln_shift


def rope_tables(prefix_len, seq):
    tok = jnp.arange(seq, dtype=jnp.int32)[None, :]
    pre = prefix_len[:, None]
    inside = tok < pre
    pos = jnp.where(inside, tok, pre - 1)
    blk = jnp.where(inside, 0, tok - pre + 1)
    inv_freq = ROT_BASE ** (-jnp.arange(QUARTER, dtype=F32) / QUARTER)
    angles = jnp.stack([pos, blk], axis=-1).astype(F32)[..., None] * inv_freq
    cos, sin = jnp.cos(angles), jnp.sin(angles)
    shape = pos.shape + (HEAD,)
    return (jnp.stack([cos, cos], axis=-2).reshape(shape), jnp.stack([-sin, sin], axis=-2).reshape(shape))


def turn(x, cos, sin):
    lane = lax.broadcasted_iota(jnp.int32, x.shape, 1)
    other = jnp.where(lane % (2 * QUARTER) < QUARTER, pltpu.roll(x, HEAD - QUARTER, 1), pltpu.roll(x, QUARTER, 1))
    return x * cos + other * sin


def qkv_kernel(me_ref, n_ref, w_ref, b_ref, cos_ref, sin_ref, q_ref, k_ref, v_ref):
    rows = cos_ref.shape[1]
    x = n_ref[...].reshape(rows, n_ref.shape[-1])
    cos, sin = cos_ref[0], sin_ref[0]
    pre = dot(x, w_ref[...], 1, 0) + b_ref[...].astype(F32)
    for h in range(q_ref.shape[0]):
        base = 3 * h * HEAD
        q_ref[h, 0] = turn(pre[:, base:base + HEAD], cos, sin).astype(BF16)
        k_ref[h, 0] = turn(pre[:, base + HEAD:base + 2 * HEAD], cos, sin).astype(BF16)
        v_ref[h, 0] = pre[:, base + 2 * HEAD:base + 3 * HEAD].astype(BF16)


def project_qkv(me, n_all, w_qkv, b_qkv, cos, sin):
    n_dev, batch, local_len, hidden = n_all.shape
    seq = n_dev * local_len
    cols = w_qkv.shape[1] // n_dev
    own = cols // (3 * HEAD)
    per = 2
    rows = per * local_len
    out = jax.ShapeDtypeStruct((own, batch, seq, HEAD), BF16)
    out_spec = pl.BlockSpec((own, 1, rows, HEAD), lambda b, j, me: (0, b, j, 0))
    tab_spec = pl.BlockSpec((1, rows, HEAD), lambda b, j, me: (b, j, 0))
    return pl.pallas_call(
        qkv_kernel,
        grid_spec=pltpu.PrefetchScalarGridSpec(
            num_scalar_prefetch=1,
            grid=(batch, n_dev // per),
            in_specs=[
                pl.BlockSpec((per, 1, local_len, hidden), lambda b, j, me: (j, b, 0, 0)),
                pl.BlockSpec((hidden, cols), lambda b, j, me: (0, me[0])),
                pl.BlockSpec((1, cols), lambda b, j, me: (0, me[0])),
                tab_spec, tab_spec,
            ],
            out_specs=[out_spec] * 3,
        ),
        out_shape=[out] * 3,
        compiler_params=pltpu.CompilerParams(vmem_limit_bytes=56 * MIB),
        cost_estimate=cost(2 * batch * seq * hidden * cols, 2 * (batch * seq * hidden + hidden * cols + batch * seq * cols)),
        name='qkv',
    )(me, n_all, w_qkv, b_qkv.reshape(1, -1), cos, sin)


def forward_kernel(pre_ref, q_ref, k_ref, v_ref, ctx_ref, lse_ref):
    seq = q_ref.shape[2]
    local_len = ctx_ref.shape[2]
    per = BLK // local_len
    prefix = pre_ref[pl.program_id(1)]

    def block(r, n_key):
        q_blk = q_ref[0, 0, r * BLK:(r + 1) * BLK]
        query = lax.broadcasted_iota(jnp.int32, (1, BLK), 1) + r * BLK
        last = jnp.maximum(query, prefix - 1)
        parts = []
        for c in range(n_key):
            part = dot(k_ref[0, 0, c * BLK:(c + 1) * BLK], q_blk, 1, 1) * (SCALE * LOG2E)
            if c >= r:
                key = lax.broadcasted_iota(jnp.int32, (BLK, BLK), 0) + c * BLK
                part = jnp.where(key <= last, part, MASK_FILL)
            parts.append(part)
        top = functools.reduce(jnp.maximum, [jnp.max(p, axis=0, keepdims=True) for p in parts])
        parts = [jnp.exp2(p - top) for p in parts]
        total = functools.reduce(jnp.add, [jnp.sum(p, axis=0, keepdims=True) for p in parts])
        inv = 1.0 / total
        probs = jnp.concatenate([(p * inv).astype(BF16) for p in parts], axis=0)
        ctx_t = dot(v_ref[0, 0, :n_key * BLK], probs, 0, 0)
        ctx_ref[r * per:(r + 1) * per, 0] = ctx_t.T.astype(BF16).reshape(per, local_len, HEAD)
        lse_ref[0, 0, :, r * BLK:(r + 1) * BLK] = top + jnp.log2(total)

    n_blk = seq // BLK
    for r in range(n_blk):
        for n_key in range(r + 1, n_blk + 1):
            low = (n_key - 1) * BLK
            cond = prefix <= n_key * BLK if n_key == r + 1 else prefix > low
            if n_key < n_blk and n_key > r + 1:
                cond = jnp.logical_and(cond, prefix <= n_key * BLK)
            if n_key == n_blk and n_key == r + 1:
                block(r, n_key)
            else:
                pl.when(cond)(functools.partial(block, r, n_key))


def attention_forward(prefix_len, q, k, v, n_dev):
    own, batch, seq, _ = q.shape
    local_len = seq // n_dev
    qkv_spec = pl.BlockSpec((1, 1, seq, HEAD), lambda h, b, pre: (h, b, 0, 0))
    return pl.pallas_call(
        forward_kernel,
        grid_spec=pltpu.PrefetchScalarGridSpec(
            num_scalar_prefetch=1,
            grid=(own, batch),
            in_specs=[qkv_spec] * 3,
            out_specs=[
                pl.BlockSpec((n_dev, 1, local_len, HEAD), lambda h, b, pre: (0, b, 0, h)),
                pl.BlockSpec((1, 1, 1, seq), lambda h, b, pre: (h, b, 0, 0)),
            ],
        ),
        out_shape=[
            jax.ShapeDtypeStruct((n_dev, batch, local_len, own * HEAD), BF16),
            jax.ShapeDtypeStruct((own, batch, 1, seq), F32),
        ],
        compiler_params=pltpu.CompilerParams(vmem_limit_bytes=32 * MIB),
        cost_estimate=cost(8 * own * batch * seq * seq * HEAD, 8 * own * batch * seq * HEAD, own * batch * seq * seq),
        name='attn_fwd',
    )(prefix_len, q, k, v)


def backward_kernel(pre_ref, q_ref, k_ref, v_ref, ctx_ref, dctx_ref, lse_ref, cos_ref, sin_ref, g_ref, sum_ref, dq_acc, dk_acc, dv_acc):
    seq = q_ref.shape[2]
    n_dev, _, local_len, _ = g_ref.shape
    n_blk = seq // BLK
    prefix = pre_ref[pl.program_id(0)]
    d_ctx = dctx_ref[...].reshape(seq, HEAD)
    prod = d_ctx.astype(F32) * ctx_ref[...].reshape(seq, HEAD).astype(F32)
    delta = jnp.sum(prod.T, axis=0, keepdims=True)

    def block(c, first):
        keys = k_ref[0, 0, c * BLK:(c + 1) * BLK]
        vals = v_ref[0, 0, c * BLK:(c + 1) * BLK]
        start = first * BLK
        q_part = q_ref[0, 0, start:]
        g_part = d_ctx[start:]
        s_t = dot(keys, q_part, 1, 1)
        dp_t = dot(vals, g_part, 1, 1)
        probs, d_scores = [], []
        for r in range(first, n_blk):
            lo = r * BLK
            piece = s_t[:, lo - start:lo - start + BLK] * (SCALE * LOG2E)
            if r <= c:
                key = lax.broadcasted_iota(jnp.int32, (BLK, BLK), 0) + c * BLK
                query = lax.broadcasted_iota(jnp.int32, (1, BLK), 1) + lo
                piece = jnp.where(key <= jnp.maximum(query, prefix - 1), piece, MASK_FILL)
            p = jnp.exp2(piece - lse_ref[0, 0, :, lo:lo + BLK])
            probs.append(p.astype(BF16))
            d_p = dp_t[:, lo - start:lo - start + BLK] - delta[:, lo:lo + BLK]
            d_scores.append((p * d_p * SCALE).astype(BF16))
        probs = jnp.concatenate(probs, axis=1)
        d_scores = jnp.concatenate(d_scores, axis=1)
        dv_acc[c * BLK:(c + 1) * BLK] = dot(probs, g_part, 1, 0)
        dk_acc[c * BLK:(c + 1) * BLK] = dot(d_scores, q_part, 1, 0)
        dq_part = dot(keys, d_scores, 0, 0)
        if c == 0:
            dq_acc[...] = dq_part
        else:
            dq_acc[:, start:] += dq_part

    block(0, 0)
    for c in range(1, n_blk):
        pl.when(prefix > c * BLK)(functools.partial(block, c, 0))
        pl.when(prefix <= c * BLK)(functools.partial(block, c, c))

    cos, sin = cos_ref[0], sin_ref[0]
    g_q = turn(dq_acc[...].T.astype(BF16).astype(F32), cos, -sin)
    g_k = turn(dk_acc[...].astype(BF16).astype(F32), cos, -sin)
    g_v = dv_acc[...].astype(BF16).astype(F32)
    for i, g in enumerate((g_q, g_k, g_v)):
        g_ref[:, 0, :, i * HEAD:(i + 1) * HEAD] = g.astype(BF16).reshape(n_dev, local_len, HEAD)
        sum_ref[0, :, i * HEAD:(i + 1) * HEAD] = jnp.sum(g, axis=0, keepdims=True)


def attention_backward(head, prefix_len, q, k, v, ctx, d_ctx, lse, cos, sin):
    _, batch, seq, _ = q.shape
    n_dev, _, local_len, _ = ctx.shape
    qkv_spec = pl.BlockSpec((1, 1, seq, HEAD), lambda b, pre: (head, b, 0, 0))
    tok_spec = pl.BlockSpec((n_dev, 1, local_len, HEAD), lambda b, pre: (0, b, 0, head))
    tab_spec = pl.BlockSpec((1, seq, HEAD), lambda b, pre: (b, 0, 0))
    return pl.pallas_call(
        backward_kernel,
        grid_spec=pltpu.PrefetchScalarGridSpec(
            num_scalar_prefetch=1,
            grid=(batch,),
            in_specs=[qkv_spec] * 3 + [tok_spec, tok_spec, pl.BlockSpec((1, 1, 1, seq), lambda b, pre: (head, b, 0, 0)), tab_spec, tab_spec],
            out_specs=[
                pl.BlockSpec((n_dev, 1, local_len, 3 * HEAD), lambda b, pre: (0, b, 0, 0)),
                pl.BlockSpec((1, 1, 3 * HEAD), lambda b, pre: (b, 0, 0)),
            ],
            scratch_shapes=[pltpu.VMEM((HEAD, seq), F32), pltpu.VMEM((seq, HEAD), F32), pltpu.VMEM((seq, HEAD), F32)],
        ),
        out_shape=[
            jax.ShapeDtypeStruct((n_dev, batch, local_len, 3 * HEAD), BF16),
            jax.ShapeDtypeStruct((batch, 1, 3 * HEAD), F32),
        ],
        compiler_params=pltpu.CompilerParams(vmem_limit_bytes=40 * MIB),
        cost_estimate=cost(20 * batch * seq * seq * HEAD, 20 * batch * seq * HEAD, batch * seq * seq),
        name='attn_bwd',
    )(prefix_len, q, k, v, ctx, d_ctx, lse, cos, sin)


def wo_grad_kernel(ctx_ref, dy_ref, out_ref):
    out_ref[...] = dot(ctx_ref[0], dy_ref[...], 0, 0)


def weight_grad_o(ctx_all, dy_all):
    n_dev, tokens, cols = ctx_all.shape
    hidden = dy_all.shape[1]
    wide = hidden // 4
    return pl.pallas_call(
        wo_grad_kernel,
        grid=(hidden // wide, n_dev),
        in_specs=[
            pl.BlockSpec((1, tokens, cols), lambda n, d: (d, 0, 0)),
            pl.BlockSpec((tokens, wide), lambda n, d: (0, n)),
        ],
        out_specs=pl.BlockSpec((cols, wide), lambda n, d: (d, n)),
        out_shape=jax.ShapeDtypeStruct((n_dev * cols, hidden), F32),
        compiler_params=pltpu.CompilerParams(vmem_limit_bytes=56 * MIB),
        cost_estimate=cost(2 * tokens * n_dev * cols * hidden, 2 * 4 * tokens * n_dev * cols + 2 * tokens * hidden + 4 * hidden * n_dev * cols),
        name='wo_grad',
    )(ctx_all, dy_all)


def wqkv_grad_kernel(head, wide, n_ref, g_ref, *rest):
    out_ref, rhs, buf, sems = rest[-4:]
    half, m = pl.program_id(0), pl.program_id(1)
    n_m = pl.num_programs(1)
    group, _, cols = g_ref.shape
    rows = n_ref.shape[1]
    step = half * n_m + m
    slot = lax.rem(step, 2)

    def copies(at_step, at_slot):
        h, r = at_step // n_m, lax.rem(at_step, n_m)
        for d in range(group):
            col = (h * group + d) * wide + head * cols
            yield pltpu.make_async_copy(
                buf.at[at_slot, :, pl.ds(d * cols, cols)],
                out_ref.at[pl.ds(pl.multiple_of(r * rows, rows), rows), pl.ds(pl.multiple_of(col, HEAD), cols)],
                sems.at[at_slot, d])

    @pl.when(m == 0)
    def _():
        for d in range(group):
            rhs[:, d * cols:(d + 1) * cols] = g_ref[d]

    @pl.when(step >= 2)
    def _():
        for c in copies(step - 2, slot):
            c.wait()

    buf[slot] = dot(n_ref[...], rhs[...], 0, 0)
    for c in copies(step, slot):
        c.start()

    @pl.when(step == 2 * n_m - 1)
    def _():
        for c in copies(step - 1, 1 - slot):
            c.wait()
        for c in copies(step, slot):
            c.wait()


def weight_grad_qkv(head, own, n_flat, g_all, partial):
    tokens, hidden = n_flat.shape
    n_dev, _, cols = g_all.shape
    group = n_dev // 2
    wide = own * cols
    rows = BLK
    any_spec = pl.BlockSpec(memory_space=pl.ANY)
    args, specs, alias = [n_flat, g_all], [
        pl.BlockSpec((tokens, rows), lambda s, m: (0, m)),
        pl.BlockSpec((group, tokens, cols), lambda s, m: (s, 0, 0)),
    ], {}
    if partial is not None:
        args.append(partial)
        specs.append(any_spec)
        alias = {2: 0}
    return pl.pallas_call(
        functools.partial(wqkv_grad_kernel, head, wide),
        grid=(2, hidden // rows),
        in_specs=specs,
        out_specs=any_spec,
        out_shape=jax.ShapeDtypeStruct((hidden, n_dev * wide), F32),
        scratch_shapes=[
            pltpu.VMEM((tokens, group * cols), BF16),
            pltpu.VMEM((2, rows, group * cols), F32),
            pltpu.SemaphoreType.DMA((2, group)),
        ],
        input_output_aliases=alias,
        compiler_params=pltpu.CompilerParams(vmem_limit_bytes=60 * MIB),
        cost_estimate=cost(2 * tokens * hidden * n_dev * cols, 4 * tokens * hidden + 2 * n_dev * tokens * cols + 4 * hidden * n_dev * cols),
        name='wqkv_grad',
    )(*args)


def solution(mesh):
    n_dev = mesh.shape['sp']
    tok_spec = P('dp', 'sp', None)
    pos_spec = P('dp', 'sp')
    in_specs = (tok_spec, pos_spec, pos_spec, P('dp'), P(), P(), P(), P(), P(), P(), tok_spec)
    out_specs = (tok_spec, tok_spec, P('dp'), P('dp'), P('dp', None), P('dp'), P('dp', None), P('dp'))

    def device_step(hidden_in, pos_ids, block_pos, prefix_len, ln_gamma, ln_beta, w_qkv, b_qkv, w_o, b_o, grad_out):
        batch, local_len, hidden = hidden_in.shape
        own = hidden // HEAD // n_dev
        rows = batch * local_len
        tokens = n_dev * rows
        rank = lax.axis_index('sp')
        me = rank.reshape(1).astype(jnp.int32)
        normed_f, norm_vjp = jax.vjp(layer_norm, hidden_in.astype(F32), ln_gamma.astype(F32), ln_beta.astype(F32))
        normed = normed_f.astype(BF16)
        n_all = lax.all_gather(normed, 'sp')
        dy_all = lax.all_gather(grad_out, 'sp')
        cos, sin = rope_tables(prefix_len, n_dev * local_len)

        q, k, v = project_qkv(me, n_all, w_qkv, b_qkv, cos, sin)
        ctx, lse = attention_forward(prefix_len, q, k, v, n_dev)
        ctx_all = lax.all_gather(ctx.reshape(tokens, own * HEAD), 'sp')

        w_o_own = lax.dynamic_slice_in_dim(w_o, rank * (own * HEAD), own * HEAD, axis=0)
        d_ctx = jnp.einsum('dbtc,hc->dbth', dy_all, w_o_own, preferred_element_type=F32).astype(BF16)
        g_parts, g_sums = [], []
        for head in range(own):
            g, g_sum = attention_backward(head, prefix_len, q, k, v, ctx, d_ctx, lse, cos, sin)
            g_parts.append(lax.all_gather(g.reshape(tokens, 3 * HEAD), 'sp'))
            g_sums.append(jnp.sum(g_sum, axis=(0, 1)))
        grad_bqkv = lax.all_gather(jnp.concatenate(g_sums), 'sp').reshape(-1)

        dy_flat = dy_all.reshape(tokens, hidden)
        grad_bo = jnp.sum(dy_flat.astype(F32), axis=0)
        grad_wo = weight_grad_o(ctx_all, dy_flat)
        ctx_tok = lax.dynamic_slice_in_dim(ctx_all, rank * rows, rows, axis=1)
        ctx_tok = jnp.transpose(ctx_tok, (1, 0, 2)).reshape(batch, local_len, hidden)
        out_f = jnp.einsum('bsh,hc->bsc', ctx_tok, w_o, preferred_element_type=F32) + b_o.astype(F32)
        hidden_out = (ALPHA * normed.astype(F32) + out_f).astype(BF16)

        n_flat = n_all.reshape(tokens, hidden)
        grad_wqkv = None
        for head in range(own):
            grad_wqkv = weight_grad_qkv(head, own, n_flat, g_parts[head], grad_wqkv)

        g_tok = [lax.dynamic_slice_in_dim(g, rank * rows, rows, axis=1) for g in g_parts]
        g_tok = jnp.transpose(jnp.stack(g_tok, axis=1), (2, 0, 1, 3)).reshape(batch, local_len, 3 * hidden)
        d_norm = jnp.einsum('bsc,hc->bsh', g_tok, w_qkv, preferred_element_type=F32) + ALPHA * grad_out.astype(F32)
        d_x, grad_gamma, grad_beta = norm_vjp(d_norm)
        grad_gamma, grad_beta = lax.psum((grad_gamma, grad_beta), 'sp')
        return (hidden_out, d_x.astype(BF16), grad_gamma, grad_beta, grad_wqkv, grad_bqkv, grad_wo, grad_bo)

    return jax.shard_map(device_step, mesh=mesh, in_specs=in_specs, out_specs=out_specs, check_vma=False)
```

time: 4530 us -> 1730 us (0.38)
  waiting for transfers between devices: 3100 us -> 570 us
  Pallas kernels: 0 us -> 826 us
  matrix products: 798 us -> 118 us
  local copies, waits for them, and re-layouts: 408 us -> 111 us
  other arithmetic: 151 us -> 45.1 us
    psum x3 -> x0, waiting for transfers between devices: 2850 us -> none  [device_step(): lax.psum((grad_gamma, grad_beta, grad_wqkv, grad_bqkv, grad_wo, grad_bo),...]
    pallas_call x0 -> x11, Pallas kernels: none -> 826 us  [the longest x4 491 us: weight_grad_qkv(): pl.pallas_call(functools.partial(wqkv_grad_kernel, head, wide), grid=(2,...]
    dot_general x118 -> x3, matrix products: 798 us -> 118 us  [the longest x1 67 us: device_step(): jnp.einsum('bsc,hc->bsh', g_tok, w_qkv, preferred_element_type=F32)]
    all_gather x0 -> x7, waiting for transfers between devices: none -> 570 us  [the longest x4 389 us: device_step(): g_parts.append(lax.all_gather(g.reshape(tokens, 3 * HEAD), 'sp'))]
    all_to_all x4 -> x0, waiting for transfers between devices: 248 us -> none  [the longest x1 130 us: device_step(): qkv_head = lax.all_to_all(qkv_tok, 'sp', 2, 1, tiled=True)]
    unnamed x66 -> x64, local copies, waits for them, and re-layouts: 182 us -> 23.1 us
  transfers between devices with their start and end apart: 7 -> 7, of which waited for: 4 -> 6; matrix products, arithmetic and copies ran while one was open for 18% -> 10% of each run, Pallas kernels for 0% -> 38%
where the time goes in v1:
time: 1730 us; the launch traced here: 1720 us
  Pallas kernels  826 us (48%)
  waiting for transfers between devices  570 us (33%)
  matrix products  118 us (7%)
  local copies, waits for them, and re-layouts  111 us (6%)
  other arithmetic  45.1 us (3%)
  blocking collectives  33.1 us (2%)
    pallas_call x4, Pallas kernels, weight_grad_qkv(): pl.pallas_call(functools.partial(wqkv_grad_kernel, head, wide), grid=(2,...  491 us
    all_gather x4, waiting for transfers between devices, device_step(): g_parts.append(lax.all_gather(g.reshape(tokens, 3 * HEAD), 'sp'))  389 us
    pallas_call x1, Pallas kernels, weight_grad_o(): pl.pallas_call(wo_grad_kernel, grid=(hidden // wide, n_dev), in_specs=[pl...  154 us
    all_gather x1, waiting for transfers between devices, device_step(): n_all = lax.all_gather(normed, 'sp')  145 us
    pallas_call x4, Pallas kernels, attention_backward(): pl.pallas_call(backward_kernel, grid_spec=pltpu.PrefetchScalarGridSpec(nu...  67.8 us
    dot_general x1, matrix products, device_step(): jnp.einsum('bsc,hc->bsh', g_tok, w_qkv, preferred_element_type=F32)  67 us
    pallas_call x1, Pallas kernels, project_qkv(): pl.pallas_call(qkv_kernel, grid_spec=pltpu.PrefetchScalarGridSpec(num_sca...  63.8 us
    pallas_call x1, Pallas kernels, attention_forward(): pl.pallas_call(forward_kernel, grid_spec=pltpu.PrefetchScalarGridSpec(num...  49.5 us
  transfers between devices with their start and end apart: 7, of which 6 were waited for; matrix products, arithmetic and copies ran while one was open for 10% of the time, Pallas kernels for 38%

profile of v1, /device:TPU:1, one launch (start us, length us, event | category | flops | bytes accessed | tf_op | source)
XLA Modules:
  0.0 1718.0 jit_solution(16335636249106865489)
XLA Ops:
  7.2 3.0 convert_reduce_fusion.1
  10.2 3.4 fusion.13
  14.8 3.3 fusion.11
  19.2 3.7 fusion.25
  24.7 3.4 copy.34.cos_ref
  28.1 1.8 copy.35.sin_ref
  30.6 145.2 %all-gather.22.cloned.1.call-done = bf16[32,128,4096]{2,1,0:T(8,128)(2,1)} async-done(((bf16[4,128,4096]{2,1,0:T(8,128)(2,1)}), bf16[32,128,4096]{2,1,0:T(8,128)(2,1)}) %all-gather.22.cloned.1.call-update) | async-done | bytes 33554448 | tf_op jit(solution)/shard_map/all_gather | solution.py:357
  175.8 63.8 %qkv.1 = (bf16[4,4,1024,128]{3,2,1,0:T(8,128)(2,1)}, bf16[4,4,1024,128]{3,2,1,0:T(8,128)(2,1)}, bf16[4,4,1024,128]{3,2,1,0:T(8,128)(2,1)}) custom-call(s32[1]{0:T(128)} %bitcast.me_ref, bf16[8,4,128,4096]{3,2,1,0:T(8,128)(2,1)} %bitcast.50, bf16[4096,12288]{1,0:T(8,128)(2,1)} %w_ref.1, bf16[1,12288]{1,0:T(2,128)(2,1)} %reshape.251.b_ref, ...), custom_call_target="tpu_custom_call" | custom-call | flops 51539607552 | bytes 58720256 | tf_op jit(solution)/shard_map/qkv/pallas_call | solution.py:80
  239.6 2.2 copy-done.7
  241.8 2.2 copy-done.12
  244.0 2.2 copy-done.13
  246.2 49.5 %attn_fwd.1 = (bf16[8,4,128,512]{3,2,1,0:T(8,128)(2,1)S(1)}, f32[4,4,1,1024]{3,2,1,0:T(1,128)S(1)}) custom-call(s32[4]{0:T(128)S(1)} %copy-done.6, bf16[4,4,1024,128]{3,2,1,0:T(8,128)(2,1)S(1)} %copy-done.7, bf16[4,4,1024,128]{3,2,1,0:T(8,128)(2,1)S(1)} %copy-done.12, bf16[4,4,1024,128]{3,2,1,0:T(8,128)(2,1)S(1)} %copy-done.13), custom_call_target="tpu_custom_call" | custom-call | flops 17179869184 | bytes 16777216 | tf_op jit(solution)/shard_map/attn_fwd/pallas_call | solution.py:143
  295.7 2.0 copy-done
  297.7 35.2 %all-gather.24.cloned.1.call-done = bf16[32,128,4096]{2,1,0:T(8,128)(2,1)} async-done(((bf16[4,128,4096]{2,1,0:T(8,128)(2,1)}), bf16[32,128,4096]{2,1,0:T(8,128)(2,1)}) %all-gather.24.cloned.1.call-update) | async-done | bytes 33554448 | tf_op jit(solution)/shard_map/all_gather | solution.py:358
  332.9 24.1 %convert_bitcast_fusion.dctx_ref = bf16[8,4,128,512]{3,2,1,0:T(8,128)(2,1)} fusion(bf16[8,4,128,4096]{3,2,1,0:T(8,128)(2,1)} %bitcast.55, bf16[4096,4096]{1,0:T(8,128)(2,1)} %param.17, s32[]{:T(128)S(6)} %select_n.36), kind=kOutput, calls=%fused_computation.25 | convolution fusion | flops 17181966336 | bytes 41943044 | tf_op jit(solution)/shard_map/dbtc,hc->dbth/dot_general | solution.py:366
  357.0 16.9 attn_bwd.4
  375.5 2.2 copy-done.9
  377.7 17.0 attn_bwd.5
  396.3 2.2 copy-done.10
  398.5 16.8 attn_bwd.6
  417.0 2.2 copy-done.11
  419.2 17.2 attn_bwd.7
  437.2 10.4 all-gather.3
  447.6 12.3 convert_reduce_fusion
  459.8 34.6 %all-gather.14.cloned.1.call-done.g_ref = bf16[8,4096,384]{2,1,0:T(8,128)(2,1)} async-done(((bf16[1,4096,384]{2,1,0:T(8,128)(2,1)}), bf16[8,4096,384]{2,1,0:T(8,128)(2,1)}) %all-gather.14.cloned.1.call-update) | async-done | bytes 25165840 | tf_op jit(solution)/shard_map/all_gather | solution.py:370
  494.4 2.3 dynamic-slice_bitcast_fusion.4
  496.7 119.1 %all-gather.16.cloned.1.call-done.g_ref = bf16[8,4096,384]{2,1,0:T(8,128)(2,1)} async-done(((bf16[1,4096,384]{2,1,0:T(8,128)(2,1)}), bf16[8,4096,384]{2,1,0:T(8,128)(2,1)}) %all-gather.16.cloned.1.call-update) | async-done | bytes 25165840 | tf_op jit(solution)/shard_map/all_gather | solution.py:370
  615.8 3.9 dynamic-slice_bitcast_fusion.3
  619.6 117.5 %all-gather.18.cloned.1.call-done.g_ref = bf16[8,4096,384]{2,1,0:T(8,128)(2,1)} async-done(((bf16[1,4096,384]{2,1,0:T(8,128)(2,1)}), bf16[8,4096,384]{2,1,0:T(8,128)(2,1)}) %all-gather.18.cloned.1.call-update) | async-done | bytes 25165840 | tf_op jit(solution)/shard_map/all_gather | solution.py:370
  737.1 3.9 dynamic-slice_bitcast_fusion.2
  741.0 118.0 %all-gather.20.cloned.1.call-done.g_ref = bf16[8,4096,384]{2,1,0:T(8,128)(2,1)} async-done(((bf16[1,4096,384]{2,1,0:T(8,128)(2,1)}), bf16[8,4096,384]{2,1,0:T(8,128)(2,1)}) %all-gather.20.cloned.1.call-update) | async-done | bytes 25165840 | tf_op jit(solution)/shard_map/all_gather | solution.py:370
  859.0 2.4 dynamic-slice_bitcast_fusion.1
  862.8 2.7 maximum_bitcast_fusion
  865.5 34.2 %copy.46 = bf16[512,8,4,384]{3,2,1,0:T(4,128)(2,1)} copy(bf16[512,8,4,384]{3,0,1,2:T(8,128)(2,1)S(1)} %maximum_bitcast_fusion) | data formatting | bytes 25165824 | tf_op jit(solution)/shard_map/transpose | solution.py:388
  899.7 20.6 %reshape.255 = bf16[4,128,12288]{2,1,0:T(8,128)(2,1)} reshape(bf16[512,8,4,384]{3,2,1,0:T(4,128)(2,1)} %copy.46) | data formatting | bytes 25165824 | tf_op jit(solution)/shard_map/reshape | solution.py:388
  920.3 67.0 %fusion.28 = (f32[4096]{0:T(1024)S(1)}, f32[4,128]{1,0:T(4,128)S(1)}, f32[4,128,4096]{2,1,0:T(8,128)}) fusion(f32[4096]{0:T(1024)S(1)} %copy-done.18, f32[4,128]{1,0:T(4,128)S(1)} %copy-done.21, bf16[4,128,4096]{2,1,0:T(8,128)(2,1)} %param.11, bf16[4,128,4096]{2,1,0:T(8,128)(2,1)} %param.19, bf16[4,128,12288]{2,1,0:T(8,128)(2,1)} %reshape.255, ...), kind=kOutput, calls=%fused_computation.50 | convolution fusion | flops 51558477824 | bytes 130060288 | tf_op jit(solution)/shard_map/bsc,hc->bsh/dot_general | solution.py:389
  987.4 6.4 fusion.12
  993.7 22.8 %all-reduce = (f32[4096]{0:T(1024)}, f32[4096]{0:T(1024)}) all-reduce(f32[4096]{0:T(1024)S(1)} %get-tuple-element.34, f32[4096]{0:T(1024)S(1)} %get-tuple-element.36), channel_id=1, replica_groups=mesh['dp'=1,'sp'=8] {'sp'}, use_global_device_ids=true, to_apply=%region_5.6 | all-reduce | flops 8192 | bytes 65536 | tf_op jit(solution)/shard_map/psum | solution.py:391
  1016.5 7.7 add_convert_fusion
  1024.2 122.6 %wqkv_grad.4.rest_0_ = f32[4096,12288]{1,0:T(8,128)} custom-call(bf16[4096,4096]{1,0:T(8,128)(2,1)} %bitcast.51, bf16[8,4096,384]{2,1,0:T(8,128)(2,1)} %all-gather.14.cloned.1.call-done.g_ref), custom_call_target="tpu_custom_call" | custom-call | flops 103079215104 | bytes 142606336 | tf_op jit(solution)/shard_map/wqkv_grad/pallas_call | solution.py:323
  1146.8 122.6 %wqkv_grad.5.rest_0_ = f32[4096,12288]{1,0:T(8,128)} custom-call(bf16[4096,4096]{1,0:T(8,128)(2,1)} %bitcast.52, bf16[8,4096,384]{2,1,0:T(8,128)(2,1)} %all-gather.16.cloned.1.call-done.g_ref, f32[4096,12288]{1,0:T(8,128)} %wqkv_grad.4.rest_0_), custom_call_target="tpu_custom_call", output_to_operand_aliasing={{}: (2, {})} | custom-call | flops 103079215104 | bytes 142606336 | tf_op jit(solution)/shard_map/wqkv_grad/pallas_call | solution.py:323
  1269.4 122.9 %wqkv_grad.6.rest_0_ = f32[4096,12288]{1,0:T(8,128)} custom-call(bf16[4096,4096]{1,0:T(8,128)(2,1)} %bitcast.53, bf16[8,4096,384]{2,1,0:T(8,128)(2,1)} %all-gather.18.cloned.1.call-done.g_ref, f32[4096,12288]{1,0:T(8,128)} %wqkv_grad.5.rest_0_), custom_call_target="tpu_custom_call", output_to_operand_aliasing={{}: (2, {})} | custom-call | flops 103079215104 | bytes 142606336 | tf_op jit(solution)/shard_map/wqkv_grad/pallas_call | solution.py:323
  1392.3 122.6 %wqkv_grad.7 = f32[4096,12288]{1,0:T(8,128)} custom-call(bf16[4096,4096]{1,0:T(8,128)(2,1)} %bitcast.54, bf16[8,4096,384]{2,1,0:T(8,128)(2,1)} %all-gather.20.cloned.1.call-done.g_ref, f32[4096,12288]{1,0:T(8,128)} %wqkv_grad.6.rest_0_), custom_call_target="tpu_custom_call", output_to_operand_aliasing={{}: (2, {})} | custom-call | flops 103079215104 | bytes 142606336 | tf_op jit(solution)/shard_map/wqkv_grad/pallas_call | solution.py:323
  1515.0 2.7 dynamic-slice_bitcast_fusion
  1517.7 4.4 copy.36
  1522.1 7.4 reshape.254
  1529.5 27.0 %add_convert_fusion.1 = bf16[4,128,4096]{2,1,0:T(8,128)(2,1)} fusion(bf16[4,128,4096]{2,1,0:T(8,128)(2,1)} %fusion.11, bf16[4,128,4096]{2,1,0:T(8,128)(2,1)} %reshape.254, bf16[4096,4096]{1,0:T(8,128)(2,1)} %param.17, f32[4096]{0:T(1024)S(1)} %copy-done.27), kind=kOutput, calls=%fused_computation.22 | convolution fusion | flops 17190354944 | bytes 46153728 | tf_op jit(solution)/shard_map/bsh,hc->bsc/dot_general | solution.py:379
  1556.6 153.8 %wo_grad.1 = f32[4096,4096]{1,0:T(8,128)} custom-call(bf16[8,4096,512]{2,1,0:T(8,128)(2,1)} %all-gather.12.cloned.1.call-done.ctx_ref, bf16[4096,4096]{1,0:T(8,128)(2,1)} %bitcast.57), custom_call_target="tpu_custom_call" | custom-call | flops 137438953472 | bytes 234881024 | tf_op jit(solution)/shard_map/wo_grad/pallas_call | solution.py:253
  (90 shorter events, 12.4 us)
Async XLA Ops:
  7.2 6.5 copy-start.28
  7.2 7.1 copy-start.29
  7.2 168.6 %all-gather.22.cloned.1.call-start = ((), (), s32[]{:S(2)}) async-start(), calls=%async_computation.5 | async-start | bytes 37748736 | tf_op jit(solution)/shard_map/all_gather | solution.py:357
  7.2 7.6 copy-start.14
  10.2 4.0 copy-start.20
  13.6 0.6 copy-start.25
  13.7 0.6 copy-start.22
  14.2 0.6 copy-start.17
  14.8 4.2 copy-start.6
  18.2 314.7 %all-gather.24.cloned.1.call-start = ((), (), s32[]{:S(2)}) async-start(), calls=%async_computation.6 | async-start | bytes 37748736 | tf_op jit(solution)/shard_map/all_gather | solution.py:358
  19.0 475.5 %all-gather.14.cloned.1.call-start = ((), (), s32[]{:S(2)}) async-start(), calls=%async_computation.1 | async-start | bytes 28311552 | tf_op jit(solution)/shard_map/all_gather | solution.py:370
  22.9 7.0 copy-start.24
  239.6 2.2 copy-start.7
  241.8 2.2 copy-start.12
  244.0 2.2 copy-start.13
  295.7 2.0 copy-start
  332.9 24.1 %copy-start.1 = (f32[4,1024,128]{2,1,0:T(8,128)S(1)}, f32[4,1024,128]{2,1,0:T(8,128)}, u32[]{:S(2)}) copy-start(f32[4,1024,128]{2,1,0:T(8,128)} %copy.34.cos_ref) | copy-start | bytes 6291460
  332.9 24.1 %copy-start.2 = (f32[4,1024,128]{2,1,0:T(8,128)S(1)}, f32[4,1024,128]{2,1,0:T(8,128)}, u32[]{:S(2)}) copy-start(f32[4,1024,128]{2,1,0:T(8,128)} %copy.35.sin_ref) | copy-start | bytes 6291460
  332.9 24.1 %copy-start.8 = (bf16[4,4,1024,128]{3,2,1,0:T(8,128)(2,1)S(1)}, bf16[4,4,1024,128]{3,2,1,0:T(8,128)(2,1)}, u32[]{:S(2)}) copy-start(bf16[4,4,1024,128]{3,2,1,0:T(8,128)(2,1)} %get-tuple-element.21.q_ref) | copy-start | bytes 12582916
  373.9 241.9 %all-gather.16.cloned.1.call-start = ((), (), s32[]{:S(2)}) async-start(), calls=%async_computation.2 | async-start | bytes 28311552 | tf_op jit(solution)/shard_map/all_gather | solution.py:370
  373.9 1.6 copy-start.3
  375.5 2.2 copy-start.9
  394.7 342.4 %all-gather.18.cloned.1.call-start = ((), (), s32[]{:S(2)}) async-start(), calls=%async_computation.3 | async-start | bytes 28311552 | tf_op jit(solution)/shard_map/all_gather | solution.py:370
  394.8 1.6 copy-start.4
  396.3 2.2 copy-start.10
  415.3 443.7 %all-gather.20.cloned.1.call-start = ((), (), s32[]{:S(2)}) async-start(), calls=%async_computation.4 | async-start | bytes 28311552 | tf_op jit(solution)/shard_map/all_gather | solution.py:370
  415.4 1.6 copy-start.5
  417.0 2.2 copy-start.11
  419.2 17.2 %copy-start.30 = (bf16[4096]{0:T(1024)(128)(2,1)S(1)}, bf16[4096]{0:T(1024)(128)(2,1)}, u32[]{:S(2)}) copy-start(bf16[4096]{0:T(1024)(128)(2,1)} %param.18) | copy-start | bytes 24580
  436.4 1078.6 %all-gather.12.cloned.1.call-start = ((), (), s32[]{:S(2)}) async-start(), calls=%async_computation | async-start | bytes 37748736 | tf_op jit(solution)/shard_map/all_gather | solution.py:363
  859.0 2.8 copy-start.15
  859.0 3.8 copy-start.16
  899.7 20.6 %copy-start.18 = (f32[4096]{0:T(1024)S(1)}, f32[4096]{0:T(1024)}, u32[]{:S(2)}) copy-start(f32[4096]{0:T(1024)} %copy-done.17) | copy-start | bytes 49156
  899.7 20.6 %copy-start.21 = (f32[4,128]{1,0:T(4,128)S(1)}, f32[4,128]{1,0:T(4,128)}, u32[]{:S(2)}) copy-start(f32[4,128]{1,0:T(4,128)} %copy-done.20) | copy-start | bytes 6148
  920.3 67.1 %copy-start.26 = (f32[4,128]{1,0:T(4,128)S(1)}, f32[4,128]{1,0:T(4,128)}, u32[]{:S(2)}) copy-start(f32[4,128]{1,0:T(4,128)} %copy-done.25) | copy-start | bytes 6148
  920.3 67.1 %copy-start.23 = (f32[4,128]{1,0:T(4,128)S(1)}, f32[4,128]{1,0:T(4,128)}, u32[]{:S(2)}) copy-start(f32[4,128]{1,0:T(4,128)} %copy-done.22) | copy-start | bytes 6148
  1517.7 11.8 copy-start.27
  1556.6 153.8 %copy-start.19 = (f32[8,1,1536]{2,1,0:T(1,128)S(1)}, f32[8,1,1536]{2,1,0:T(1,128)}, u32[]{:S(2)}) copy-start(f32[8,1,1536]{2,1,0:T(1,128)} %all-gather.3) | copy-start | bytes 147460
Sparse Core Ops, SparseCore 0:
  18.3 157.4 all-gather.21
  177.6 155.2 all-gather.23
  374.0 120.3 all-gather.13
  496.1 119.6 all-gather.15
  617.4 119.6 all-gather.17
  739.3 119.6 all-gather.19
  860.8 156.0 all-gather.11
